TPU v7x, 32 devices: a whole 2x2x4 slice. The times are simulated.
32 devices in a mesh: dp: 4 (over x, core), tensor: 8 (over z, y).
Axes of the slice: x: 2, y: 2, z: 4, core: 2. Of those that a mesh axis runs over, the one named last changes fastest.
Arguments:
- hidden: bfloat16 [8, 64, 4608], P('dp', 'tensor'), may hold values from -6 to 6
- gain: float32 [4608], replicated, may hold values from 0.5 to 1.5
- labels: int32 [8, 64], P('dp', 'tensor'), may hold values from 0 to 255999
- lengths: int32 [8], replicated, may hold values from 1 to 64
- embed: bfloat16 [256000, 4608], P(('dp', 'tensor')), may hold values from -0.375 to 0.375
Outputs:
- token_logprob: float32 [8, 64], P('dp', 'tensor')
- mean_nll: float32 [], replicated
- z_loss: float32 [], replicated
All inputs are finite; a program needn't handle non-finite values.
Results may differ from a plain program's by a relative error of at most 0.00058.
Values may be sent and summed in bfloat16 or wider, within the bound.
A program may use at most 128 MiB of HBM per device.

v0:
```python
import jax
import jax.numpy as jnp
from jax import lax
from jax.sharding import PartitionSpec as P

CAP = 30


def normalize(rows, gain):
    values = rows.astype(jnp.float32)
    meansq = jnp.mean(values * values, axis=-1, keepdims=True)
    return (values * lax.rsqrt(meansq + 1e-06) * gain).astype(jnp.bfloat16)


def per_device(hidden, gain, labels, lengths, embed):
    n_tensor = lax.axis_size("tensor")
    n_all = lax.axis_size("dp") * n_tensor
    seqs, stretch, width = hidden.shape
    vocab_dev = embed.shape[0]
    rows_local = seqs * stretch
    total_rows = rows_local * n_all
    flat = hidden.reshape(rows_local, width)
    row_ids = jnp.arange(total_rows)
    owner = row_ids // rows_local
    within = row_ids % rows_local
    batch_ids = owner // n_tensor * seqs + within // stretch
    positions = owner % n_tensor * stretch + within % stretch
    live_all = (positions < jnp.take(lengths, batch_ids)).astype(jnp.float32)
    all_labels = lax.all_gather(labels.reshape(rows_local), ("dp", "tensor"), axis=0, tiled=True)
    outgoing = normalize(flat, gain)
    rows = lax.all_gather(outgoing, ("dp", "tensor"), axis=0, tiled=True)
    values = lax.dot_general(
        rows, embed, (((1,), (1,)), ((), ())), preferred_element_type=jnp.float32
    )
    capped = CAP * jnp.tanh(values / CAP)
    sumexp = jnp.sum(jnp.exp(capped), axis=1)
    first = lax.axis_index(("dp", "tensor")) * vocab_dev
    local = all_labels - first
    inside = (local >= 0) & (local < vocab_dev)
    chosen = jnp.take_along_axis(capped, jnp.clip(local, 0, vocab_dev - 1)[:, None], axis=1)[:, 0]
    picked = jnp.where(inside, chosen, jnp.float32(0.0))
    own_start = lax.axis_index(("dp", "tensor")) * rows_local
    sum_total, pick_total = lax.psum((sumexp, picked), ("dp", "tensor"))
    own_sum = lax.dynamic_slice_in_dim(sum_total, own_start, rows_local)
    own_pick = lax.dynamic_slice_in_dim(pick_total, own_start, rows_local)
    own_live = lax.dynamic_slice_in_dim(live_all, own_start, rows_local)
    lse = jnp.log(own_sum)
    token = own_live * (own_pick - lse)
    nll_sum, count, square_sum = lax.psum(
        (-jnp.sum(token), jnp.sum(own_live), jnp.sum(own_live * lse * lse)), ("dp", "tensor")
    )
    mean_nll = nll_sum / count
    z_loss = 0.01 * square_sum / count
    return (token.reshape(seqs, stretch), mean_nll, z_loss)


def solution(mesh):
    return jax.shard_map(
        per_device,
        mesh=mesh,
        in_specs=(P("dp", "tensor", None), P(), P("dp", "tensor"), P(), P(("dp", "tensor"), None)),
        out_specs=(P("dp", "tensor"), P(), P()),
        check_vma=False,
    )
```

profile of v0, /device:TPU:0, one launch (start us, length us, event | category | flops | bytes accessed | tf_op | source)
XLA Modules:
  0.0 240.6 jit_solution(1555822703838976775)
XLA Ops:
  7.2 0.0 all-gather.2.cloned.1.call-start
  7.2 1.0 fusion.3
  8.3 0.1 rsqrt.12
  8.3 1.7 fusion.2
  10.0 0.0 all-gather.2.cloned.1.call-update
  10.0 0.8 reshape.263
  10.8 0.2 dynamic-update-slice
  11.0 42.2 %all-reduce = s32[512]{0:T(512)S(1)} all-reduce(s32[512]{0:T(512)S(1)} %dynamic-update-slice), channel_id=1, replica_groups=mesh['dp'=4,'tensor'=8] {'dp','tensor'}, use_global_device_ids=true, to_apply=%add | all-reduce | flops 512 | bytes 4096
  53.2 1.6 fusion.29
  54.8 4.5 %compare_select_fusion.1 = s32[512,1]{0,1:T(1,128)S(1)} fusion(s32[]{:T(128)} %bitcast.1, s32[]{:T(128)} %bitcast.2, s32[]{:T(128)} %bitcast.3, s32[]{:T(128)} %bitcast.4, s32[]{:T(128)} %bitcast.5, s32[]{:T(128)} %bitcast.7, s32[]{:T(128)} %bitcast.6), kind=kLoop, calls=%fused_computation.11 | loop fusion | flops 30208 | bytes 2076 | tf_op jit(solution)/shard_map/jit(_take)/gather | solution.py:28
  59.4 0.7 fusion.26
  60.1 17.2 %all-gather.2.cloned.1.call-done = bf16[512,4608]{1,0:T(8,128)(2,1)} async-done(((bf16[16,4608]{1,0:T(8,128)(2,1)}), bf16[512,4608]{1,0:T(8,128)(2,1)}) %all-gather.2.cloned.1.call-update) | async-done | bytes 4718608 | tf_op jit(solution)/shard_map/all_gather | solution.py:31
  77.3 48.5 %exponential_reduce_fusion = (f32[512]{0:T(512)S(1)}, f32[512,8000]{0,1:T(8,128)}) fusion(bf16[512,4608]{1,0:T(8,128)(2,1)} %all-gather.2.cloned.1.call-done, bf16[8000,4608]{1,0:T(8,128)(2,1)} %param.9), kind=kOutput, calls=%fused_computation.1 | convolution fusion | flops 37761024000 | bytes 94832640 | tf_op jit(solution)/shard_map/dot_general | solution.py:32
  125.8 22.4 %gather_fusion = f32[512]{0:T(512)S(1)} fusion(f32[512,8000]{0,1:T(8,128)} %get-tuple-element.23, s32[512]{0:T(512)S(1)} %bitcast.23), kind=kCustom, calls=%fused_computation | custom fusion | bytes 8192 | tf_op jit(solution)/shard_map/jit(take_along_axis)/gather | solution.py:40
  148.2 37.6 %all-reduce.2 = (f32[512]{0:T(512)S(1)}, f32[512]{0:T(512)S(1)}) all-reduce(f32[512]{0:T(512)S(1)} %select_select_fusion.1, f32[512]{0:T(512)S(1)} %get-tuple-element.22), channel_id=1, replica_groups=mesh['dp'=4,'tensor'=8] {'dp','tensor'}, use_global_device_ids=true, to_apply=%region_1.2 | all-reduce | flops 1024 | bytes 8192 | tf_op jit(solution)/shard_map/psum | solution.py:43
  185.8 0.8 fusion.27
  186.6 0.6 reshape.216
  187.9 41.0 %all-reduce.1 = (f32[]{:T(128)}, f32[]{:T(128)}, f32[]{:T(128)}) all-reduce(f32[]{:T(128)S(6)} %neg.3, f32[]{:T(128)} %get-tuple-element.4, f32[]{:T(128)} %get-tuple-element.3), channel_id=1, replica_groups=mesh['dp'=4,'tensor'=8] {'dp','tensor'}, use_global_device_ids=true, to_apply=%region_5.6 | all-reduce | flops 3 | bytes 24 | tf_op jit(solution)/shard_map/psum | solution.py:49
  (8 shorter events, 0.1 us)
Async XLA Ops:
  7.2 70.1 %all-gather.2.cloned.1.call-start = ((), (), s32[]{:S(2)}) async-start(), calls=%async_computation | async-start | bytes 4866048 | tf_op jit(solution)/shard_map/all_gather | solution.py:31
Sparse Core Ops, SparseCore 0:
  10.9 66.3 all-gather.1
where the time goes:
time: 241 us
  blocking collectives  121 us (50%)
  matrix products  48.5 us (20%)
  local copies, waits for them, and re-layouts  25.7 us (11%)
  between operations  19.6 us (8%)
  waiting for transfers between devices  17.2 us (7%)
  other arithmetic  8.75 us (4%)
    dot_general x1, matrix products, per_device(): lax.dot_general(rows, embed, (((1,), (1,)), ((), ())), preferred_element_...  48.5 us
    unnamed x1, blocking collectives  42.2 us
    psum x1, blocking collectives, per_device(): lax.psum((-jnp.sum(token), jnp.sum(own_live), jnp.sum(own_live * lse * ls...  41 us
    psum x1, blocking collectives, per_device(): sum_total, pick_total = lax.psum((sumexp, picked), ('dp', 'tensor'))  37.6 us
    gather x1, local copies, waits for them, and re-layouts, per_device(): jnp.take_along_axis(capped, jnp.clip(local, 0, vocab_dev - 1)[:, None], a...  22.4 us
    all_gather x1, waiting for transfers between devices, per_device(): rows = lax.all_gather(outgoing, ('dp', 'tensor'), axis=0, tiled=True)  17.2 us
  transfers between devices with their start and end apart: 1, of which 1 were waited for; matrix products, arithmetic and copies ran while one was open for 3% of the time, Pallas kernels for 0%

commit v1 on v0

--- a/solution.py
+++ b/solution.py
@@ -2,6 +2,7 @@
 import jax.numpy as jnp
 from jax import lax
 from jax.sharding import PartitionSpec as P
+from jax.lax import psum
 
 CAP = 30
 
@@ -40,7 +41,11 @@
     chosen = jnp.take_along_axis(capped, jnp.clip(local, 0, vocab_dev - 1)[:, None], axis=1)[:, 0]
     picked = jnp.where(inside, chosen, jnp.float32(0.0))
     own_start = lax.axis_index(("dp", "tensor")) * rows_local
-    sum_total, pick_total = lax.psum((sumexp, picked), ("dp", "tensor"))
+
+    def point_local_data_by_axis(sample):
+        return psum(psum(sample, axis_name="tensor"), axis_name="dp")
+
+    sum_total, pick_total = point_local_data_by_axis((sumexp, picked))
     own_sum = lax.dynamic_slice_in_dim(sum_total, own_start, rows_local)
     own_pick = lax.dynamic_slice_in_dim(pick_total, own_start, rows_local)
     own_live = lax.dynamic_slice_in_dim(live_all, own_start, rows_local)

time: 241 us -> 224 us (0.929)
  blocking collectives: 121 us -> 103 us
    psum x1 -> x2, blocking collectives: 37.6 us -> 23.7 us  [point_local_data_by_axis(): return psum(psum(sample, axis_name='tensor'), axis_name='dp')]
    psum x1, blocking collectives: 41 us -> 37.1 us  [per_device(): lax.psum((-jnp.sum(token), jnp.sum(own_live), jnp.sum(own_live * lse * ls...]
  transfers between devices with their start and end apart: 1 -> 1, of which waited for: 1 -> 1; matrix products, arithmetic and copies ran while one was open for 3% -> 4% of each run, Pallas kernels for 0% -> 0%
where the time goes in v1:
time: 224 us; the launch traced here: 223 us
  blocking collectives  103 us (46%)
  matrix products  48.5 us (22%)
  local copies, waits for them, and re-layouts  25.7 us (11%)
  between operations  19.6 us (9%)
  waiting for transfers between devices  17.2 us (8%)
  other arithmetic  8.75 us (4%)
    dot_general x1, matrix products, per_device(): lax.dot_general(rows, embed, (((1,), (1,)), ((), ())), preferred_element_...  48.5 us
    unnamed x1, blocking collectives  42.2 us
    psum x1, blocking collectives, per_device(): lax.psum((-jnp.sum(token), jnp.sum(own_live), jnp.sum(own_live * lse * ls...  37.1 us
    psum x2, blocking collectives, point_local_data_by_axis(): return psum(psum(sample, axis_name='tensor'), axis_name='dp')  23.7 us
    gather x1, local copies, waits for them, and re-layouts, per_device(): jnp.take_along_axis(capped, jnp.clip(local, 0, vocab_dev - 1)[:, None], a...  22.4 us
    all_gather x1, waiting for transfers between devices, per_device(): rows = lax.all_gather(outgoing, ('dp', 'tensor'), axis=0, tiled=True)  17.2 us
    gather x2, other arithmetic, per_device(): live_all = (positions < jnp.take(lengths, batch_ids)).astype(jnp.float32)  4.56 us
  transfers between devices with their start and end apart: 1, of which 1 were waited for; matrix products, arithmetic and copies ran while one was open for 4% of the time, Pallas kernels for 0%

profile of v1, /device:TPU:0, one launch (start us, length us, event | category | flops | bytes accessed | tf_op | source)
XLA Modules:
  0.0 222.8 jit_solution(1924517840298856229)
XLA Ops:
  7.2 0.0 all-gather.2.cloned.1.call-start
  7.2 1.0 fusion.3
  8.3 0.1 rsqrt.12
  8.3 1.7 fusion.2
  10.0 0.0 all-gather.2.cloned.1.call-update
  10.0 0.8 reshape.263
  10.8 0.2 dynamic-update-slice
  11.0 42.2 %all-reduce = s32[512]{0:T(512)S(1)} all-reduce(s32[512]{0:T(512)S(1)} %dynamic-update-slice), channel_id=1, replica_groups=mesh['dp'=4,'tensor'=8] {'dp','tensor'}, use_global_device_ids=true, to_apply=%add | all-reduce | flops 512 | bytes 4096
  53.2 1.6 fusion.29
  54.8 4.5 %compare_select_fusion.1 = s32[512,1]{0,1:T(1,128)S(1)} fusion(s32[]{:T(128)} %bitcast.1, s32[]{:T(128)} %bitcast.2, s32[]{:T(128)} %bitcast.3, s32[]{:T(128)} %bitcast.4, s32[]{:T(128)} %bitcast.5, s32[]{:T(128)} %bitcast.7, s32[]{:T(128)} %bitcast.6), kind=kLoop, calls=%fused_computation.11 | loop fusion | flops 30208 | bytes 2076 | tf_op jit(solution)/shard_map/jit(_take)/gather | solution.py:29
  59.4 0.7 fusion.26
  60.1 17.2 %all-gather.2.cloned.1.call-done = bf16[512,4608]{1,0:T(8,128)(2,1)} async-done(((bf16[16,4608]{1,0:T(8,128)(2,1)}), bf16[512,4608]{1,0:T(8,128)(2,1)}) %all-gather.2.cloned.1.call-update) | async-done | bytes 4718608 | tf_op jit(solution)/shard_map/all_gather | solution.py:32
  77.3 48.5 %exponential_reduce_fusion = (f32[512]{0:T(512)S(1)}, f32[512,8000]{0,1:T(8,128)}) fusion(bf16[512,4608]{1,0:T(8,128)(2,1)} %all-gather.2.cloned.1.call-done, bf16[8000,4608]{1,0:T(8,128)(2,1)} %param.9), kind=kOutput, calls=%fused_computation.1 | convolution fusion | flops 37761024000 | bytes 94832640 | tf_op jit(solution)/shard_map/dot_general | solution.py:33
  125.8 22.4 %gather_fusion = f32[512]{0:T(512)S(1)} fusion(f32[512,8000]{0,1:T(8,128)} %get-tuple-element.25, s32[512]{0:T(512)S(1)} %bitcast.23), kind=kCustom, calls=%fused_computation | custom fusion | bytes 8192 | tf_op jit(solution)/shard_map/jit(take_along_axis)/gather | solution.py:41
  148.2 17.9 %all-reduce.2 = (f32[512]{0:T(512)S(1)}, f32[512]{0:T(512)S(1)}) all-reduce(f32[512]{0:T(512)S(1)} %select_select_fusion.1, f32[512]{0:T(512)S(1)} %get-tuple-element.24), channel_id=1, replica_groups=mesh['dp'=4,'tensor'=8] {'tensor'}, use_global_device_ids=true, to_apply=%region_1.2 | all-reduce | flops 1024 | bytes 8192 | tf_op jit(solution)/shard_map/psum | solution.py:46
  166.1 5.7 %all-reduce.3 = (f32[512]{0:T(512)S(1)}, f32[512]{0:T(512)S(1)}) all-reduce(f32[512]{0:T(512)S(1)} %get-tuple-element.8, f32[512]{0:T(512)S(1)} %get-tuple-element.9), channel_id=1, replica_groups=mesh['dp'=4,'tensor'=8] {'dp'}, use_global_device_ids=true, to_apply=%region_2.3 | all-reduce | flops 1024 | bytes 8192 | tf_op jit(solution)/shard_map/psum | solution.py:46
  171.9 0.8 fusion.27
  172.6 0.6 reshape.216
  174.0 37.1 %all-reduce.1 = (f32[]{:T(128)}, f32[]{:T(128)}, f32[]{:T(128)}) all-reduce(f32[]{:T(128)S(6)} %neg.3, f32[]{:T(128)} %get-tuple-element.4, f32[]{:T(128)} %get-tuple-element.3), channel_id=1, replica_groups=mesh['dp'=4,'tensor'=8] {'dp','tensor'}, use_global_device_ids=true, to_apply=%region_7.8 | all-reduce | flops 3 | bytes 24 | tf_op jit(solution)/shard_map/psum | solution.py:54
  (8 shorter events, 0.1 us)
Async XLA Ops:
  7.2 70.1 %all-gather.2.cloned.1.call-start = ((), (), s32[]{:S(2)}) async-start(), calls=%async_computation | async-start | bytes 4866048 | tf_op jit(solution)/shard_map/all_gather | solution.py:32
Sparse Core Ops, SparseCore 0:
  10.9 66.3 all-gather.1
